TPU v7x, 32 devices: a whole 2x2x4 slice. The times are simulated.
32 devices in a mesh: cluster: 4 (over y, x), member: 8 (over z, core).
Axes of the slice: x: 2, y: 2, z: 4, core: 2. Of those that a mesh axis runs over, the one named last changes fastest.
Arguments:
- embeddings: bfloat16 [8192, 4096], P(('cluster', 'member')), may hold values from -15 to 15, as said below
- start_basis: bfloat16 [4096, 512], P(('cluster', 'member')), may hold values from -6 to 6
- cluster_ids: int32 [8192], P(('cluster', 'member')), may hold values from 0 to 7
- valid_counts: int32 [4], P('cluster'), may hold values from 512 to 2048
Outputs:
- subspace: float32 [4096, 512], P(('cluster', 'member'))
- nearest: float32 [8192], P(('cluster', 'member'))
Inputs may be any that keep to these rules, and one draw needn't show every extreme that they name: `embeddings`: Real-valued entries.
All inputs are finite; a program needn't handle non-finite values.
Results may differ from a plain program's by a relative error of at most 0.0042.
Values may be sent and summed in bfloat16 or wider, within the bound.
No kernel may reach another device: no remote copies, remote signals or barrier semaphores. Data moves between devices by JAX's collectives and lax.ppermute only.
A program may use at most 64 MiB of HBM per device.

v0:
```python
import math
import jax
import jax.numpy as jnp
from jax import lax
from jax.sharding import PartitionSpec as P

D = 4096
ITERS = 2
EPS = 1e-06


def spread_basis(local_rows):
    return lax.all_gather(local_rows, ("cluster", "member"), axis=0, tiled=True)


def reduce_image(centered, projected):
    return lax.psum_scatter(
        lax.dot_general(
            centered, projected, (((0,), (0,)), ((), ())), preferred_element_type=jnp.float32
        ),
        ("cluster", "member"),
        scatter_dimension=0,
        tiled=True,
    )


def body(embeddings, start_basis, cluster_ids, valid_counts):
    row_count = embeddings.shape[0]
    total_rows = row_count * lax.axis_size(("cluster", "member"))
    ones_row = jnp.ones((1, row_count), jnp.bfloat16)
    column_sums = jnp.dot(ones_row, embeddings, preferred_element_type=jnp.float32)[0]
    average = lax.psum(column_sums, ("cluster", "member")) / total_rows
    centered = (embeddings.astype(jnp.float32) - average).astype(jnp.bfloat16)
    basis_full = spread_basis(start_basis)
    orthonormal = None
    for sweep in range(ITERS):
        projected = jnp.dot(centered, basis_full, preferred_element_type=jnp.float32).astype(
            jnp.bfloat16
        )
        image = reduce_image(centered, projected) / total_rows
        local_gram = jnp.dot(image.T, image, precision=lax.Precision.HIGHEST)
        gram = lax.psum(local_gram, ("cluster", "member"))
        lower = jnp.linalg.cholesky(gram)
        orthonormal = jax.scipy.linalg.solve_triangular(lower, image.T, lower=True).T
        basis_full = spread_basis(orthonormal.astype(jnp.bfloat16))
    subspace = orthonormal * math.sqrt(D)
    coords = jnp.dot(centered, basis_full, preferred_element_type=jnp.float32)
    unit = (coords * lax.rsqrt(jnp.sum(coords * coords, axis=1, keepdims=True) + EPS)).astype(
        jnp.bfloat16
    )
    label_values = cluster_ids.astype(jnp.bfloat16)
    limit = valid_counts[0]
    own_index = lax.axis_index("member") * row_count + jnp.arange(row_count, dtype=jnp.int32)
    initial = jnp.full((row_count,), -1.0, jnp.float32)
    piece_units = lax.all_gather(unit, "member", axis=0, tiled=True)
    piece_labels = lax.all_gather(label_values, "member", axis=0, tiled=True)
    scores = lax.dot_general(
        unit, piece_units, (((1,), (1,)), ((), ())), preferred_element_type=jnp.float32
    )
    others = jnp.arange(piece_units.shape[0], dtype=jnp.int32)
    allowed = (
        (label_values[:, None] == piece_labels[None, :])
        & (others[None, :] < limit)
        & (others[None, :] != own_index[:, None])
    )
    nearest = jnp.maximum(initial, jnp.max(jnp.where(allowed, scores, -1.0), axis=1))
    return (subspace, nearest)


def solution(mesh):
    placed = (
        P(("cluster", "member"), None),
        P(("cluster", "member"), None),
        P(("cluster", "member")),
        P("cluster"),
    )
    return jax.shard_map(
        body,
        mesh=mesh,
        in_specs=placed,
        out_specs=(P(("cluster", "member"), None), P(("cluster", "member"))),
        check_vma=False,
    )
```

profile of v0, /device:TPU:0, one launch (start us, length us, event | category | flops | bytes accessed | tf_op | source)
XLA Modules:
  0.0 1155.7 jit_solution(3383755361846079378)
XLA Ops:
  9.9 42.8 %psum.21 = f32[4096]{0:T(1024)S(1)} all-reduce(f32[4096]{0:T(1024)S(1)} %bitcast.117), channel_id=1, replica_groups=mesh['cluster'=4,'member'=8] {'cluster','member'}, use_global_device_ids=true, to_apply=%region_0.0 | all-reduce | flops 4096 | bytes 32768 | tf_op jit(solution)/shard_map/psum | solution.py:32
  52.8 22.7 %all-gather.6.cloned.1.call-done = bf16[4096,512]{1,0:T(8,128)(2,1)} async-done(((bf16[128,512]{1,0:T(8,128)(2,1)}), bf16[4096,512]{1,0:T(8,128)(2,1)}) %all-gather.6.cloned.1.call-update) | async-done | bytes 4194320 | tf_op jit(solution)/shard_map/all_gather | solution.py:13
  83.4 153.1 %reduce-scatter.3.cloned.1.call-done = f32[128,512]{1,0:T(8,128)} async-done(((f32[4096,512]{1,0:T(8,128)}), f32[128,512]{1,0:T(8,128)}) %reduce-scatter.3.cloned.1.call-update) | async-done | bytes 262160 | tf_op jit(solution)/shard_map/reduce_scatter | solution.py:17
  240.5 129.6 %all-reduce.4.cloned.1.call-done = f32[512,512]{0,1:T(8,128)} async-done(((f32[512,512]{0,1:T(8,128)}), f32[512,512]{0,1:T(8,128)}) %all-reduce.4.cloned.1.call-update) | async-done | bytes 1048592 | tf_op jit(solution)/shard_map/psum | solution.py:42
  375.3 11.7 %cholesky.286 = f32[128,128]{1,0:T(8,128)S(1)} custom-call(f32[128,128]{1,0:T(8,128)S(1)} %cholesky.426), custom_call_target="Cholesky" | custom-call | tf_op jit(solution)/shard_map/jit(cholesky)/cholesky | solution.py:43
  400.7 11.7 %cholesky.305 = f32[128,128]{1,0:T(8,128)S(1)} custom-call(f32[128,128]{1,0:T(8,128)S(1)} %cholesky.430), custom_call_target="Cholesky" | custom-call | tf_op jit(solution)/shard_map/jit(cholesky)/cholesky | solution.py:43
  412.9 10.3 custom-call.28
  426.3 13.2 %cholesky.326 = f32[128,128]{1,0:T(8,128)} custom-call(f32[128,128]{1,0:T(8,128)} %cholesky.435), custom_call_target="Cholesky" | custom-call | tf_op jit(solution)/shard_map/jit(cholesky)/cholesky | solution.py:43
  441.6 11.3 custom-call.29
  455.1 11.7 %cholesky.343 = f32[128,128]{1,0:T(8,128)S(1)} custom-call(f32[128,128]{1,0:T(8,128)S(1)} %convolution_subtract_fusion.11), custom_call_target="Cholesky" | custom-call | tf_op jit(solution)/shard_map/jit(cholesky)/cholesky | solution.py:43
  472.6 12.0 %while.4 = (s32[]{:T(128)}, f32[512,512]{1,0:T(8,128)}, s32[4,2]{0,1:T(2,128)S(1)}, f32[4,128,128]{2,1,0:T(8,128)S(1)}, s32[]{:T(128)}) while((s32[]{:T(128)}, f32[512,512]{1,0:T(8,128)}, s32[4,2]{0,1:T(2,128)S(1)}, f32[4,128,128]{2,1,0:T(8,128)S(1)}, s32[]{:T(128)}) %tuple.59), condition=%wide.while_cond, body=%wide.while_body.sunk | while | flops 2 | bytes 131181 | solution.py:44
  485.2 39.3 %custom-call.30 = f32[4,128,128]{1,2,0:T(8,128)S(1)} custom-call(f32[4,128,128]{2,1,0:T(8,128)S(1)} %get-tuple-element.18), custom_call_target="InvertDiagBlocksLowerTriangular" | custom-call | tf_op jit(solution)/shard_map/jit(_solve_triangular)/triangular_solve | solution.py:44
  530.3 64.1 %all-gather.8.cloned.1.call-done = bf16[4096,512]{0,1:T(8,128)(2,1)} async-done(((bf16[128,512]{0,1:T(8,128)(2,1)}), bf16[4096,512]{0,1:T(8,128)(2,1)}) %all-gather.8.cloned.1.call-update) | async-done | bytes 4194320 | tf_op jit(solution)/shard_map/all_gather | solution.py:13
  602.5 152.4 %reduce-scatter.5.cloned.1.call-done = f32[128,512]{1,0:T(8,128)} async-done(((f32[4096,512]{1,0:T(8,128)}), f32[128,512]{1,0:T(8,128)}) %reduce-scatter.5.cloned.1.call-update) | async-done | bytes 262160 | tf_op jit(solution)/shard_map/reduce_scatter | solution.py:17
  758.4 130.1 %all-reduce.6.cloned.1.call-done = f32[512,512]{0,1:T(8,128)} async-done(((f32[512,512]{0,1:T(8,128)}), f32[512,512]{0,1:T(8,128)}) %all-reduce.6.cloned.1.call-update) | async-done | bytes 1048592 | tf_op jit(solution)/shard_map/psum | solution.py:42
  893.6 11.7 %cholesky.358 = f32[128,128]{1,0:T(8,128)S(1)} custom-call(f32[128,128]{1,0:T(8,128)S(1)} %cholesky.439), custom_call_target="Cholesky" | custom-call | tf_op jit(solution)/shard_map/jit(cholesky)/cholesky | solution.py:43
  919.1 11.7 %cholesky.377 = f32[128,128]{1,0:T(8,128)S(1)} custom-call(f32[128,128]{1,0:T(8,128)S(1)} %cholesky.443), custom_call_target="Cholesky" | custom-call | tf_op jit(solution)/shard_map/jit(cholesky)/cholesky | solution.py:43
  946.1 13.2 %cholesky.398 = f32[128,128]{1,0:T(8,128)} custom-call(f32[128,128]{1,0:T(8,128)} %cholesky.448), custom_call_target="Cholesky" | custom-call | tf_op jit(solution)/shard_map/jit(cholesky)/cholesky | solution.py:43
  961.5 11.3 custom-call.33
  975.0 12.3 %cholesky.415 = f32[128,128]{1,0:T(8,128)} custom-call(f32[128,128]{1,0:T(8,128)S(1)} %convolution_subtract_fusion.9), custom_call_target="Cholesky" | custom-call | tf_op jit(solution)/shard_map/jit(cholesky)/cholesky | solution.py:43
  992.7 11.6 %while.5 = (s32[]{:T(128)}, f32[512,512]{1,0:T(8,128)}, s32[4,2]{0,1:T(2,128)S(1)}, f32[4,128,128]{2,1,0:T(8,128)S(1)}, s32[]{:T(128)}) while((s32[]{:T(128)}, f32[512,512]{1,0:T(8,128)}, s32[4,2]{0,1:T(2,128)S(1)}, f32[4,128,128]{2,1,0:T(8,128)S(1)}, s32[]{:T(128)}) %tuple.81), condition=%wide.while_cond.clone, body=%wide.while_body.clone.sunk | while | flops 2 | bytes 131181 | solution.py:44
  1004.3 39.3 %custom-call.34 = f32[4,128,128]{1,2,0:T(8,128)S(1)} custom-call(f32[4,128,128]{2,1,0:T(8,128)S(1)} %get-tuple-element.19), custom_call_target="InvertDiagBlocksLowerTriangular" | custom-call | tf_op jit(solution)/shard_map/jit(_solve_triangular)/triangular_solve | solution.py:44
  1049.4 64.1 %all-gather.10.cloned.1.call-done = bf16[4096,512]{0,1:T(8,128)(2,1)} async-done(((bf16[128,512]{0,1:T(8,128)(2,1)}), bf16[4096,512]{0,1:T(8,128)(2,1)}) %all-gather.10.cloned.1.call-update) | async-done | bytes 4194320 | tf_op jit(solution)/shard_map/all_gather | solution.py:13
  1129.4 16.0 %all-gather.12.cloned.1.call-done = bf16[2048,512]{1,0:T(8,128)(2,1)} async-done(((bf16[256,512]{1,0:T(8,128)(2,1)}), bf16[2048,512]{1,0:T(8,128)(2,1)}) %all-gather.12.cloned.1.call-update) | async-done | bytes 2097168 | tf_op jit(solution)/shard_map/all_gather | solution.py:55
  (152 shorter events, 151.3 us)
Async XLA Ops:
  7.2 68.3 %copy-start = (bf16[256,4096]{1,0:T(8,128)(2,1)S(1)}, bf16[256,4096]{1,0:T(8,128)(2,1)}, u32[]{:S(2)}) copy-start(bf16[256,4096]{1,0:T(8,128)(2,1)} %param.7) | copy-start | bytes 6291460
  7.2 68.3 %all-gather.6.cloned.1.call-start = ((), (), s32[]{:S(2)}) async-start(), calls=%async_computation.2 | async-start | bytes 4325376 | tf_op jit(solution)/shard_map/all_gather | solution.py:13
  7.9 228.5 %reduce-scatter.3.cloned.1.call-start = ((), (), s32[]{:S(2)}) async-start(), calls=%async_computation.3 | async-start | bytes 8650752 | tf_op jit(solution)/shard_map/reduce_scatter | solution.py:17
  83.3 286.8 %all-reduce.4.cloned.1.call-start = ((), (), s32[]{:S(2)}) async-start(), calls=%async_computation.4 | async-start | bytes 2097152 | tf_op jit(solution)/shard_map/psum | solution.py:42
  236.4 4.1 copy-start.5
  239.6 354.8 %all-gather.8.cloned.1.call-start = ((), (), s32[]{:S(2)}) async-start(), calls=%async_computation.5 | async-start | bytes 4325376 | tf_op jit(solution)/shard_map/all_gather | solution.py:13
  370.1 2.7 copy-start.1
  374.3 1.0 copy-start.4
  400.0 0.7 copy-start.8
  466.8 5.8 copy-start.12
  484.7 0.6 copy-start.9
  530.3 224.6 %reduce-scatter.5.cloned.1.call-start = ((), (), s32[]{:S(2)}) async-start(), calls=%async_computation.6 | async-start | bytes 8650752 | tf_op jit(solution)/shard_map/reduce_scatter | solution.py:17
  602.4 286.0 %all-reduce.6.cloned.1.call-start = ((), (), s32[]{:S(2)}) async-start(), calls=%async_computation.7 | async-start | bytes 2097152 | tf_op jit(solution)/shard_map/psum | solution.py:42
  754.9 3.5 copy-start.6
  758.1 355.5 %all-gather.10.cloned.1.call-start = ((), (), s32[]{:S(2)}) async-start(), calls=%async_computation.8 | async-start | bytes 4325376 | tf_op jit(solution)/shard_map/all_gather | solution.py:13
  888.5 2.7 copy-start.2
  892.6 1.0 copy-start.3
  918.4 0.7 copy-start.7
  973.8 18.9 %copy-start.10 = (s32[4,2]{0,1:T(2,128)S(1)}, s32[4,2]{0,1:T(2,128)}, u32[]{:S(2)}) copy-start(s32[4,2]{0,1:T(2,128)} %copy-done.9) | copy-start | bytes 100
  1049.3 68.6 %copy-start.11 = (s32[256]{0:T(256)S(1)}, s32[256]{0:T(256)}, u32[]{:S(2)}) copy-start(s32[256]{0:T(256)} %param.9) | copy-start | bytes 3076
  1049.3 96.1 %all-gather.12.cloned.1.call-start = ((), (), s32[]{:S(2)}) async-start(), calls=%async_computation.9 | async-start | bytes 2359296 | tf_op jit(solution)/shard_map/all_gather | solution.py:55
Sparse Core Ops, SparseCore 0:
  11.0 64.3 all-gather.5
  83.5 152.9 reduce-scatter.2
  241.6 128.4 all-reduce.3
  530.4 64.0 all-gather.7
  602.5 152.2 reduce-scatter.4
  759.9 128.4 all-reduce.5
  1049.4 64.0 all-gather.9
  1118.1 27.3 all-gather.11
where the time goes:
time: 1160 us
  waiting for transfers between devices  733 us (63%)
  other arithmetic  259 us (22%)
  matrix products  54.7 us (5%)
  blocking collectives  52.6 us (5%)
  local copies, waits for them, and re-layouts  35.1 us (3%)
  between operations  20.6 us (2%)
    reduce_scatter x2, waiting for transfers between devices, reduce_image(): lax.psum_scatter(lax.dot_general(centered, projected, (((0,), (0,)), ((),...  305 us
    psum x2, waiting for transfers between devices, body(): gram = lax.psum(local_gram, ('cluster', 'member'))  260 us
    another operation x29, other arithmetic, body(): lower = jnp.linalg.cholesky(gram)  172 us
    all_gather x3, waiting for transfers between devices, spread_basis(): return lax.all_gather(local_rows, ('cluster', 'member'), axis=0, tiled=True)  151 us
    another operation x5, other arithmetic, body(): jax.scipy.linalg.solve_triangular(lower, image.T, lower=True)  81.4 us
    psum x1, blocking collectives, body(): average = lax.psum(column_sums, ('cluster', 'member')) / total_rows  42.8 us
    another operation x27, local copies, waits for them, and re-layouts, body(): jax.scipy.linalg.solve_triangular(lower, image.T, lower=True)  23.5 us
  transfers between devices with their start and end apart: 8, of which 8 were waited for; matrix products, arithmetic and copies ran while one was open for 0% of the time, Pallas kernels for 0%

commit v1 on v0

--- a/solution.py
+++ b/solution.py
@@ -39,7 +39,9 @@
         )
         image = reduce_image(centered, projected) / total_rows
         local_gram = jnp.dot(image.T, image, precision=lax.Precision.HIGHEST)
-        gram = lax.psum(local_gram, ("cluster", "member"))
+        gram = local_gram
+        for mesh_axis in ("member", "cluster"):
+            gram = lax.psum(gram, mesh_axis)
         lower = jnp.linalg.cholesky(gram)
         orthonormal = jax.scipy.linalg.solve_triangular(lower, image.T, lower=True).T
         basis_full = spread_basis(orthonormal.astype(jnp.bfloat16))

time: 1160 us -> 1130 us (0.974)
  waiting for transfers between devices: 733 us -> 697 us
    psum x2 -> x4, waiting for transfers between devices: 260 us -> 222 us  [body(): gram = lax.psum(gram, mesh_axis)]
  transfers between devices with their start and end apart: 8 -> 10, of which waited for: 8 -> 10; matrix products, arithmetic and copies ran while one was open for 0% -> 0% of each run, Pallas kernels for 0% -> 0%
where the time goes in v1:
time: 1130 us; the launch traced here: 1120 us
  waiting for transfers between devices  697 us (62%)
  other arithmetic  259 us (23%)
  matrix products  54.7 us (5%)
  blocking collectives  52.7 us (5%)
  local copies, waits for them, and re-layouts  35 us (3%)
  between operations  20.6 us (2%)
    reduce_scatter x2, waiting for transfers between devices, reduce_image(): lax.psum_scatter(lax.dot_general(centered, projected, (((0,), (0,)), ((),...  305 us
    psum x4, waiting for transfers between devices, body(): gram = lax.psum(gram, mesh_axis)  222 us
    another operation x29, other arithmetic, body(): lower = jnp.linalg.cholesky(gram)  172 us
    all_gather x3, waiting for transfers between devices, spread_basis(): return lax.all_gather(local_rows, ('cluster', 'member'), axis=0, tiled=True)  153 us
    another operation x5, other arithmetic, body(): jax.scipy.linalg.solve_triangular(lower, image.T, lower=True)  81.4 us
    psum x1, blocking collectives, body(): average = lax.psum(column_sums, ('cluster', 'member')) / total_rows  42.8 us
    another operation x27, local copies, waits for them, and re-layouts, body(): jax.scipy.linalg.solve_triangular(lower, image.T, lower=True)  23.5 us
  transfers between devices with their start and end apart: 10, of which 10 were waited for; matrix products, arithmetic and copies ran while one was open for 0% of the time, Pallas kernels for 0%

profile of v1, /device:TPU:0, one launch (start us, length us, event | category | flops | bytes accessed | tf_op | source)
XLA Modules:
  0.0 1120.2 jit_solution(9118268415937341258)
XLA Ops:
  9.9 42.8 %psum.35 = f32[4096]{0:T(1024)S(1)} all-reduce(f32[4096]{0:T(1024)S(1)} %bitcast.117), channel_id=1, replica_groups=mesh['cluster'=4,'member'=8] {'cluster','member'}, use_global_device_ids=true, to_apply=%region_0.0 | all-reduce | flops 4096 | bytes 32768 | tf_op jit(solution)/shard_map/psum | solution.py:32
  52.8 22.7 %all-gather.6.cloned.1.call-done = bf16[4096,512]{1,0:T(8,128)(2,1)} async-done(((bf16[128,512]{1,0:T(8,128)(2,1)}), bf16[4096,512]{1,0:T(8,128)(2,1)}) %all-gather.6.cloned.1.call-update) | async-done | bytes 4194320 | tf_op jit(solution)/shard_map/all_gather | solution.py:13
  83.4 152.6 %reduce-scatter.3.cloned.1.call-done = f32[128,512]{1,0:T(8,128)} async-done(((f32[4096,512]{1,0:T(8,128)}), f32[128,512]{1,0:T(8,128)}) %reduce-scatter.3.cloned.1.call-update) | async-done | bytes 262160 | tf_op jit(solution)/shard_map/reduce_scatter | solution.py:17
  239.3 57.3 %all-reduce.6.cloned.1.call-done = f32[512,512]{0,1:T(8,128)} async-done(((f32[512,512]{0,1:T(8,128)}), f32[512,512]{0,1:T(8,128)}) %all-reduce.6.cloned.1.call-update) | async-done | bytes 1048592 | tf_op jit(solution)/shard_map/psum | solution.py:44
  297.5 53.6 %all-reduce.8.cloned.1.call-done = f32[512,512]{0,1:T(8,128)} async-done(((f32[512,512]{0,1:T(8,128)}), f32[512,512]{0,1:T(8,128)}) %all-reduce.8.cloned.1.call-update) | async-done | bytes 1048592 | tf_op jit(solution)/shard_map/psum | solution.py:44
  356.2 11.7 %cholesky.286 = f32[128,128]{1,0:T(8,128)S(1)} custom-call(f32[128,128]{1,0:T(8,128)S(1)} %cholesky.426), custom_call_target="Cholesky" | custom-call | tf_op jit(solution)/shard_map/jit(cholesky)/cholesky | solution.py:45
  381.6 11.7 %cholesky.305 = f32[128,128]{1,0:T(8,128)S(1)} custom-call(f32[128,128]{1,0:T(8,128)S(1)} %cholesky.430), custom_call_target="Cholesky" | custom-call | tf_op jit(solution)/shard_map/jit(cholesky)/cholesky | solution.py:45
  407.2 13.2 %cholesky.326 = f32[128,128]{1,0:T(8,128)} custom-call(f32[128,128]{1,0:T(8,128)} %cholesky.435), custom_call_target="Cholesky" | custom-call | tf_op jit(solution)/shard_map/jit(cholesky)/cholesky | solution.py:45
  422.5 11.3 %custom-call.29 = f32[1,128,128]{1,2,0:T(8,128)} custom-call(f32[1,128,128]{2,1,0:T(8,128)} %get-tuple-element.59), custom_call_target="InvertDiagBlocksLowerTriangular" | custom-call | tf_op jit(solution)/shard_map/jit(cholesky)/cholesky | solution.py:45
  436.0 11.7 %cholesky.343 = f32[128,128]{1,0:T(8,128)S(1)} custom-call(f32[128,128]{1,0:T(8,128)S(1)} %convolution_subtract_fusion.11), custom_call_target="Cholesky" | custom-call | tf_op jit(solution)/shard_map/jit(cholesky)/cholesky | solution.py:45
  453.5 12.0 %while.4 = (s32[]{:T(128)}, f32[512,512]{1,0:T(8,128)}, s32[4,2]{0,1:T(2,128)S(1)}, f32[4,128,128]{2,1,0:T(8,128)S(1)}, s32[]{:T(128)}) while((s32[]{:T(128)}, f32[512,512]{1,0:T(8,128)}, s32[4,2]{0,1:T(2,128)S(1)}, f32[4,128,128]{2,1,0:T(8,128)S(1)}, s32[]{:T(128)}) %tuple.59), condition=%wide.while_cond, body=%wide.while_body.sunk | while | flops 2 | bytes 131181 | solution.py:46
  466.1 39.3 %custom-call.30 = f32[4,128,128]{1,2,0:T(8,128)S(1)} custom-call(f32[4,128,128]{2,1,0:T(8,128)S(1)} %get-tuple-element.18), custom_call_target="InvertDiagBlocksLowerTriangular" | custom-call | tf_op jit(solution)/shard_map/jit(_solve_triangular)/triangular_solve | solution.py:46
  511.2 65.2 %all-gather.8.cloned.1.call-done = bf16[4096,512]{0,1:T(8,128)(2,1)} async-done(((bf16[128,512]{0,1:T(8,128)(2,1)}), bf16[4096,512]{0,1:T(8,128)(2,1)}) %all-gather.8.cloned.1.call-update) | async-done | bytes 4194320 | tf_op jit(solution)/shard_map/all_gather | solution.py:13
  584.4 152.6 %reduce-scatter.5.cloned.1.call-done = f32[128,512]{1,0:T(8,128)} async-done(((f32[4096,512]{1,0:T(8,128)}), f32[128,512]{1,0:T(8,128)}) %reduce-scatter.5.cloned.1.call-update) | async-done | bytes 262160 | tf_op jit(solution)/shard_map/reduce_scatter | solution.py:17
  740.2 57.1 %all-reduce.10.cloned.1.call-done = f32[512,512]{0,1:T(8,128)} async-done(((f32[512,512]{0,1:T(8,128)}), f32[512,512]{0,1:T(8,128)}) %all-reduce.10.cloned.1.call-update) | async-done | bytes 1048592 | tf_op jit(solution)/shard_map/psum | solution.py:44
  797.6 54.3 %all-reduce.12.cloned.1.call-done = f32[512,512]{0,1:T(8,128)} async-done(((f32[512,512]{0,1:T(8,128)}), f32[512,512]{0,1:T(8,128)}) %all-reduce.12.cloned.1.call-update) | async-done | bytes 1048592 | tf_op jit(solution)/shard_map/psum | solution.py:44
  857.0 11.7 %cholesky.358 = f32[128,128]{1,0:T(8,128)S(1)} custom-call(f32[128,128]{1,0:T(8,128)S(1)} %cholesky.439), custom_call_target="Cholesky" | custom-call | tf_op jit(solution)/shard_map/jit(cholesky)/cholesky | solution.py:45
  882.5 11.7 %cholesky.377 = f32[128,128]{1,0:T(8,128)S(1)} custom-call(f32[128,128]{1,0:T(8,128)S(1)} %cholesky.443), custom_call_target="Cholesky" | custom-call | tf_op jit(solution)/shard_map/jit(cholesky)/cholesky | solution.py:45
  909.5 13.2 %cholesky.398 = f32[128,128]{1,0:T(8,128)} custom-call(f32[128,128]{1,0:T(8,128)} %cholesky.448), custom_call_target="Cholesky" | custom-call | tf_op jit(solution)/shard_map/jit(cholesky)/cholesky | solution.py:45
  938.5 12.3 %cholesky.415 = f32[128,128]{1,0:T(8,128)} custom-call(f32[128,128]{1,0:T(8,128)S(1)} %convolution_subtract_fusion.9), custom_call_target="Cholesky" | custom-call | tf_op jit(solution)/shard_map/jit(cholesky)/cholesky | solution.py:45
  956.1 11.6 %while.5 = (s32[]{:T(128)}, f32[512,512]{1,0:T(8,128)}, s32[4,2]{0,1:T(2,128)S(1)}, f32[4,128,128]{2,1,0:T(8,128)S(1)}, s32[]{:T(128)}) while((s32[]{:T(128)}, f32[512,512]{1,0:T(8,128)}, s32[4,2]{0,1:T(2,128)S(1)}, f32[4,128,128]{2,1,0:T(8,128)S(1)}, s32[]{:T(128)}) %tuple.85), condition=%wide.while_cond.clone, body=%wide.while_body.clone.sunk | while | flops 2 | bytes 131181 | solution.py:46
  967.7 39.3 %custom-call.34 = f32[4,128,128]{1,2,0:T(8,128)S(1)} custom-call(f32[4,128,128]{2,1,0:T(8,128)S(1)} %get-tuple-element.19), custom_call_target="InvertDiagBlocksLowerTriangular" | custom-call | tf_op jit(solution)/shard_map/jit(_solve_triangular)/triangular_solve | solution.py:46
  1012.8 65.2 %all-gather.10.cloned.1.call-done = bf16[4096,512]{0,1:T(8,128)(2,1)} async-done(((bf16[128,512]{0,1:T(8,128)(2,1)}), bf16[4096,512]{0,1:T(8,128)(2,1)}) %all-gather.10.cloned.1.call-update) | async-done | bytes 4194320 | tf_op jit(solution)/shard_map/all_gather | solution.py:13
  1093.9 16.0 %all-gather.12.cloned.1.call-done = bf16[2048,512]{1,0:T(8,128)(2,1)} async-done(((bf16[256,512]{1,0:T(8,128)(2,1)}), bf16[2048,512]{1,0:T(8,128)(2,1)}) %all-gather.12.cloned.1.call-update) | async-done | bytes 2097168 | tf_op jit(solution)/shard_map/all_gather | solution.py:57
  (158 shorter events, 172.9 us)
Async XLA Ops:
  7.2 68.3 %copy-start = (bf16[256,4096]{1,0:T(8,128)(2,1)S(1)}, bf16[256,4096]{1,0:T(8,128)(2,1)}, u32[]{:S(2)}) copy-start(bf16[256,4096]{1,0:T(8,128)(2,1)} %param.7) | copy-start | bytes 6291460
  7.2 68.3 %all-gather.6.cloned.1.call-start = ((), (), s32[]{:S(2)}) async-start(), calls=%async_computation.2 | async-start | bytes 4325376 | tf_op jit(solution)/shard_map/all_gather | solution.py:13
  7.9 228.1 %reduce-scatter.3.cloned.1.call-start = ((), (), s32[]{:S(2)}) async-start(), calls=%async_computation.3 | async-start | bytes 8650752 | tf_op jit(solution)/shard_map/reduce_scatter | solution.py:17
  83.3 213.2 %all-reduce.6.cloned.1.call-start = ((), (), s32[]{:S(2)}) async-start(), calls=%async_computation.4 | async-start | bytes 2097152 | tf_op jit(solution)/shard_map/psum | solution.py:44
  236.0 61.4 %copy-start.5 = (f32[128,512]{1,0:T(8,128)S(1)}, f32[128,512]{1,0:T(8,128)}, u32[]{:S(2)}) copy-start(f32[128,512]{1,0:T(8,128)} %reduce-scatter.3.cloned.1.call-done) | copy-start | bytes 786436
  239.2 111.8 %all-reduce.8.cloned.1.call-start = ((), (), s32[]{:S(2)}) async-start(), calls=%async_computation.5 | async-start | bytes 2097152 | tf_op jit(solution)/shard_map/psum | solution.py:44
  296.6 279.8 %all-gather.8.cloned.1.call-start = ((), (), s32[]{:S(2)}) async-start(), calls=%async_computation.6 | async-start | bytes 4325376 | tf_op jit(solution)/shard_map/all_gather | solution.py:13
  351.1 2.6 copy-start.1
  355.2 1.0 copy-start.4
  380.9 0.7 copy-start.8
  447.7 5.8 copy-start.12
  465.6 0.6 copy-start.9
  511.2 225.8 %reduce-scatter.5.cloned.1.call-start = ((), (), s32[]{:S(2)}) async-start(), calls=%async_computation.7 | async-start | bytes 8650752 | tf_op jit(solution)/shard_map/reduce_scatter | solution.py:17
  584.4 212.9 %all-reduce.10.cloned.1.call-start = ((), (), s32[]{:S(2)}) async-start(), calls=%async_computation.8 | async-start | bytes 2097152 | tf_op jit(solution)/shard_map/psum | solution.py:44
  737.0 60.6 %copy-start.6 = (f32[128,512]{1,0:T(8,128)S(1)}, f32[128,512]{1,0:T(8,128)}, u32[]{:S(2)}) copy-start(f32[128,512]{1,0:T(8,128)} %reduce-scatter.5.cloned.1.call-done) | copy-start | bytes 786436
  740.2 111.7 %all-reduce.12.cloned.1.call-start = ((), (), s32[]{:S(2)}) async-start(), calls=%async_computation.9 | async-start | bytes 2097152 | tf_op jit(solution)/shard_map/psum | solution.py:44
  797.3 280.7 %all-gather.10.cloned.1.call-start = ((), (), s32[]{:S(2)}) async-start(), calls=%async_computation.10 | async-start | bytes 4325376 | tf_op jit(solution)/shard_map/all_gather | solution.py:13
  851.9 2.6 copy-start.2
  856.0 1.0 copy-start.3
  881.8 0.7 copy-start.7
  937.2 18.9 %copy-start.10 = (s32[4,2]{0,1:T(2,128)S(1)}, s32[4,2]{0,1:T(2,128)}, u32[]{:S(2)}) copy-start(s32[4,2]{0,1:T(2,128)} %copy-done.9) | copy-start | bytes 100
  1012.8 69.7 %copy-start.11 = (s32[256]{0:T(256)S(1)}, s32[256]{0:T(256)}, u32[]{:S(2)}) copy-start(s32[256]{0:T(256)} %param.9) | copy-start | bytes 3076
  1012.8 97.1 %all-gather.12.cloned.1.call-start = ((), (), s32[]{:S(2)}) async-start(), calls=%async_computation.11 | async-start | bytes 2359296 | tf_op jit(solution)/shard_map/all_gather | solution.py:57
Sparse Core Ops, SparseCore 0:
  11.0 64.3 all-gather.5
  83.5 152.5 reduce-scatter.2
  239.3 57.1 all-reduce.5
  299.5 51.5 all-reduce.7
  511.3 65.0 all-gather.7
  584.5 152.4 reduce-scatter.4
  740.3 56.9 all-reduce.9
  800.4 51.5 all-reduce.11
  1012.9 65.0 all-gather.9
  1082.6 27.3 all-gather.11
